TPU v7x, 128 devices: a whole 4x4x4 slice. The times are simulated.
128 devices in a mesh: box: 16 (over y, z), panel: 8 (over x, core).
Axes of the slice: x: 4, y: 4, z: 4, core: 2. Of those that a mesh axis runs over, the one named last changes fastest.
Arguments:
- field_start: float32 [4096, 4096], P('box', 'panel'), may hold values from -6 to 6
- fluid_mask: int32 [4096, 4096], P('box', 'panel'), may hold values 0 or 1
- base_visc: float32 [4096, 4096], P('box', 'panel'), may hold values from 0.02 to 0.1
- panel_cell: int32 [16384], P(('box', 'panel')), may hold values from 0 to 131071
- amplitude: bfloat16 [16384, 4096], P('box', 'panel'), may hold values from 0.049804688 to 0.5
- delay_bin: int32 [16384, 4096], P('box', 'panel'), may hold values from 0 to 2044
Outputs:
- field_end: float32 [4096, 4096], P('box', 'panel')
- signals: float32 [4096, 2048], P('panel', 'box')
Inputs may be any that keep to these rules, and one draw needn't show every extreme that they name: `panel_cell`: an index, row-major, into the 256 x 512 block of the device that owns the panel.
All inputs are finite; a program needn't handle non-finite values. No bound on the sum of `fluid_mask` on one device may be relied on, other than what follows from the above.
Results may differ from a plain program's by a relative error of at most 0.0029.
Values may be sent and summed in bfloat16 or wider, within the bound.
A program may use at most 64 MiB of HBM per device.

v0:
```python
import math
import jax
import jax.numpy as jnp
from jax import lax
from jax.sharding import PartitionSpec as P

STEPS = 4
NB = 2048


def padded(x, sides, width):
    edges = {}
    for axis, dim in sides:
        peers, length = (lax.axis_size(axis), x.shape[dim])
        up = [(i, (i + 1) % peers) for i in range(peers - 1)]
        last = lax.slice_in_dim(x, length - width, length, axis=dim)
        initial = lax.slice_in_dim(x, 0, width, axis=dim)
        edges[dim] = (
            lax.ppermute(last, axis, up),
            lax.ppermute(initial, axis, [(b, a) for a, b in up]),
        )
    done = []
    for _, dim in sides:
        low, high = edges[dim]
        around = [(width, width) if d in done else (0, 0) for d in range(x.ndim)]
        x = jnp.concatenate([jnp.pad(low, around), x, jnp.pad(high, around)], axis=dim)
        done.append(dim)
    return x


def advance(ext, mask_c, base_c):
    center = ext[1:-1, 1:-1]
    west = ext[:-2, 1:-1]
    east = ext[2:, 1:-1]
    south = ext[1:-1, :-2]
    north = ext[1:-1, 2:]
    grad_x = 0.5 * (east - west)
    grad_y = 0.5 * (north - south)
    grad_norm = jnp.sqrt(grad_x * grad_x + grad_y * grad_y)
    viscosity = base_c + 0.05 * grad_norm / (1.0 + grad_norm)
    update = center + viscosity * (east + west + north + south - 4.0 * center)
    update = update - 0.15 * (center - west) - 0.1 * (center - south)
    return mask_c * update


def signal_terms(amplitude, delay_bin, sample):
    panels, observers = amplitude.shape
    groups = NB // 128
    width = math.gcd(observers, max(1, 32768 // panels))
    blocks = observers // width
    amp_blocks = amplitude.reshape(panels, blocks, width).transpose(1, 0, 2)
    bin_blocks = delay_bin.reshape(panels, blocks, width).transpose(1, 0, 2)
    high_ids = jnp.arange(groups, dtype=jnp.int32)
    low_ids = jnp.arange(128, dtype=jnp.int32)

    def one_block(pair):
        amp_rows, bin_rows = pair
        weight = (amp_rows.astype(jnp.float32)[None, :, :] * sample[:, :, None]).astype(
            jnp.bfloat16
        )
        high = bin_rows // 128
        low = bin_rows % 128
        chosen = high[:, :, None] == high_ids[None, None, :]
        left = jnp.where(chosen[None], weight[:, :, :, None], jnp.zeros((), jnp.bfloat16))
        right = (low[:, :, None] == low_ids[None, None, :]).astype(jnp.bfloat16)
        binned = jnp.einsum("tpoh,pol->othl", left, right, preferred_element_type=jnp.float32)
        binned = binned.reshape(width, STEPS, NB)
        total = binned[:, 0, :]
        for step in range(1, STEPS):
            total = total + jnp.pad(binned[:, step, : NB - step], ((0, 0), (step, 0)))
        return total

    result = lax.map(one_block, (amp_blocks, bin_blocks))
    return result.reshape(observers, NB)


def on_device(field_start, fluid_mask, base_visc, panel_cell, amplitude, delay_bin):
    maskf = fluid_mask.astype(jnp.float32)
    taken = []
    field = field_start
    for step in range(STEPS):
        extended = padded(field, (("box", 0), ("panel", 1)), 1)
        field = advance(extended, maskf, base_visc)
        taken.append(field.reshape(-1)[panel_cell])
    sample = jnp.stack(taken)
    every = lax.all_gather(sample, ("box", "panel"), axis=1, tiled=True)
    amp_all = lax.all_to_all(amplitude, "box", split_axis=1, concat_axis=0, tiled=True)
    bin_all = lax.all_to_all(delay_bin, "box", split_axis=1, concat_axis=0, tiled=True)
    finished = signal_terms(amp_all, bin_all, every)
    signals = lax.all_to_all(finished, "box", split_axis=1, concat_axis=0, tiled=True)
    return (field, signals)


def solution(mesh):
    placed = (
        P("box", "panel"),
        P("box", "panel"),
        P("box", "panel"),
        P(("box", "panel")),
        P("box", "panel"),
        P("box", "panel"),
    )
    return jax.shard_map(
        on_device,
        mesh=mesh,
        in_specs=placed,
        out_specs=(P("box", "panel"), P("panel", "box")),
        check_vma=False,
    )
```

profile of v0, /device:TPU:0, one launch (start us, length us, event | category | flops | bytes accessed | tf_op | source)
XLA Modules:
  0.0 311.0 jit_solution(857162247917352217)
XLA Ops:
  2.8 4.6 %collective-permute-start.1 = (f32[1,512]{1,0:T(1,128)S(1)}, f32[1,512]{1,0:T(1,128)S(1)}, u32[]{:S(2)}, u32[]{:S(2)}) collective-permute-start(f32[1,512]{1,0:T(1,128)S(1)} %get-tuple-element.136), channel_id=1, source_target_pairs={{0,8},{8,16},{16,24},{24,32},{32,40},{40,48},{48,56},{56,64},{64,7... | collective-permute-start | bytes 6152 | tf_op jit(solution)/shard_map/ppermute | solution.py:19
  8.4 1.3 collective-permute-start.2
  9.7 3.0 collective-permute-start.3
  12.8 2.3 copy.28
  15.1 10.3 %all-to-all-start.1 = ((bf16[1024,16,32]{0,2,1:T(8,128)(2,1)}), bf16[1024,16,32]{0,2,1:T(8,128)(2,1)S(1)}, u32[]{:S(2)}, u32[]{:S(2)}) async-start(bf16[1024,16,32]{0,2,1:T(8,128)(2,1)} %bitcast.105), calls=%async_computation.1 | async-start | bytes 2097152 | tf_op jit(solution)/shard_map/all_to_all | solution.py:87
  26.2 1.3 collective-permute-start.4
  27.5 4.5 %collective-permute-start.5 = (f32[1,512]{1,0:T(1,128)S(1)}, f32[1,512]{1,0:T(1,128)S(1)}, u32[]{:S(2)}, u32[]{:S(2)}) collective-permute-start(f32[1,512]{1,0:T(1,128)S(1)} %get-tuple-element.132), channel_id=1, source_target_pairs={{0,8},{8,16},{16,24},{24,32},{32,40},{40,48},{48,56},{56,64},{64,7... | collective-permute-start | bytes 6152 | tf_op jit(solution)/shard_map/ppermute | solution.py:19
  32.2 1.3 collective-permute-start.6
  33.5 3.0 collective-permute-start.7
  36.5 2.9 copy.26
  43.0 4.0 %collective-permute-start.11 = (f32[256,1]{1,0:T(8,128)S(1)}, f32[256,1]{1,0:T(8,128)S(1)}, u32[]{:S(2)}, u32[]{:S(2)}) collective-permute-start(f32[256,1]{1,0:T(8,128)S(1)} %get-tuple-element.125), channel_id=1, source_target_pairs={{0,1},{1,2},{2,3},{3,4},{4,5},{5,6},{6,7},{8,9},{9,10},{10,11},{11... | collective-permute-start | bytes 3080 | tf_op jit(solution)/shard_map/ppermute | solution.py:19
  48.0 8.8 %all-to-all-start = ((s32[1024,16,32]{0,2,1:T(8,128)}), s32[1024,16,32]{0,2,1:T(8,128)S(1)}, u32[]{:S(2)}, u32[]{:S(2)}) async-start(s32[1024,16,32]{0,2,1:T(8,128)} %bitcast), calls=%async_computation | async-start | bytes 4194304 | tf_op jit(solution)/shard_map/all_to_all | solution.py:88
  58.8 4.5 %collective-permute-start.9 = (f32[1,512]{1,0:T(1,128)S(1)}, f32[1,512]{1,0:T(1,128)S(1)}, u32[]{:S(2)}, u32[]{:S(2)}) collective-permute-start(f32[1,512]{1,0:T(1,128)S(1)} %get-tuple-element.128), channel_id=1, source_target_pairs={{0,8},{8,16},{16,24},{24,32},{32,40},{40,48},{48,56},{56,64},{64,7... | collective-permute-start | bytes 6152 | tf_op jit(solution)/shard_map/ppermute | solution.py:19
  63.4 5.8 %collective-permute-done.8 = f32[1,512]{1,0:T(1,128)S(1)} collective-permute-done((f32[1,512]{1,0:T(1,128)S(1)}, f32[1,512]{1,0:T(1,128)S(1)}, u32[]{:S(2)}, u32[]{:S(2)}) %collective-permute-start.8) | collective-permute-done | bytes 2080 | tf_op jit(solution)/shard_map/ppermute | solution.py:20
  69.2 2.7 fusion.44
  72.8 1.3 collective-permute-start.14
  74.1 11.1 %collective-permute-start.15 = (f32[256,1]{1,0:T(8,128)}, f32[256,1]{1,0:T(8,128)}, u32[]{:S(2)}, u32[]{:S(2)}) collective-permute-start(f32[256,1]{1,0:T(8,128)} %get-tuple-element.121), channel_id=1, source_target_pairs={{0,1},{1,2},{2,3},{3,4},{4,5},{5,6},{6,7},{8,9},{9,10},{10,11},{11... | collective-permute-start | bytes 3080 | tf_op jit(solution)/shard_map/ppermute | solution.py:19
  87.0 4.5 %collective-permute-start.13 = (f32[1,512]{1,0:T(1,128)S(1)}, f32[1,512]{1,0:T(1,128)S(1)}, u32[]{:S(2)}, u32[]{:S(2)}) collective-permute-start(f32[1,512]{1,0:T(1,128)S(1)} %get-tuple-element.124), channel_id=1, source_target_pairs={{0,8},{8,16},{16,24},{24,32},{32,40},{40,48},{48,56},{56,64},{64,7... | collective-permute-start | bytes 6152 | tf_op jit(solution)/shard_map/ppermute | solution.py:19
  91.6 2.0 copy.36
  93.6 2.5 gather_fusion
  96.2 2.0 copy.37
  98.1 2.5 gather_fusion.1
  100.6 2.0 copy.38
  102.6 2.6 gather_fusion.2
  105.3 2.8 fusion.26
  110.9 48.7 %all_gather.3 = f32[4,16384]{1,0:T(4,128)S(1)} all-gather(f32[4,128]{1,0:T(4,128)S(1)} %pad_maximum_fusion.24), channel_id=1, replica_groups=mesh['box'=16,'panel'=8] {'box','panel'}, dimensions={1}, use_global_device_ids=true | all-gather | bytes 264192 | tf_op jit(solution)/shard_map/all_gather | solution.py:86
  159.6 2.8 copy.29
  162.4 2.6 reshape.98
  165.0 2.6 copy.27
  167.6 3.0 reshape.97
  170.6 125.7 %while.13 = (s32[]{:T(128)}, f32[16,2,2048]{2,1,0:T(2,128)S(1)}, s32[16,16384,2]{1,2,0:T(2,128)S(1)}, bf16[16,16384,2]{1,2,0:T(2,128)(2,1)}, f32[4,16384]{1,0:T(4,128)S(1)}, /*index=5*/s32[]{:T(128)}) while((s32[]{:T(128)}, f32[16,2,2048]{2,1,0:T(2,128)S(1)}, s32[16,16384,2]{1,2,0:T(2,128)S(1)}, bf16[16,16384,2]{1,2,0:T(2,128)(2,1)}, ...), condition=%wide.region_1.2_spmd.clone, body=%wide.region_0.1_spmd.clone.sunk | while | flops 544616448 | bytes 11714449 | solution.py:73
  173.2 4.9 %fusion.114 = f32[2,4,16,128]{3,2,1,0:T(8,128)S(1)} fusion(s32[16384,2]{0,1:T(2,128)S(1)} %get-tuple-element.170, bf16[4,16384,2,16]{1,3,0,2:T(8,128)(2,1)S(1)} %fusion.113), kind=kOutput, calls=%fused_computation.8.clone.3 | convolution fusion | flops 541065216 | bytes 4390912 | tf_op jit(solution)/shard_map/while/body/eval_jaxpr/tpoh,pol->othl/dot_general | solution.py:66
  181.1 4.9 %fusion.114 = f32[2,4,16,128]{3,2,1,0:T(8,128)S(1)} fusion(s32[16384,2]{0,1:T(2,128)S(1)} %get-tuple-element.170, bf16[4,16384,2,16]{1,3,0,2:T(8,128)(2,1)S(1)} %fusion.113), kind=kOutput, calls=%fused_computation.8.clone.3 | convolution fusion | flops 541065216 | bytes 4390912 | tf_op jit(solution)/shard_map/while/body/eval_jaxpr/tpoh,pol->othl/dot_general | solution.py:66
  188.9 4.9 %fusion.114 = f32[2,4,16,128]{3,2,1,0:T(8,128)S(1)} fusion(s32[16384,2]{0,1:T(2,128)S(1)} %get-tuple-element.170, bf16[4,16384,2,16]{1,3,0,2:T(8,128)(2,1)S(1)} %fusion.113), kind=kOutput, calls=%fused_computation.8.clone.3 | convolution fusion | flops 541065216 | bytes 4390912 | tf_op jit(solution)/shard_map/while/body/eval_jaxpr/tpoh,pol->othl/dot_general | solution.py:66
  196.8 4.9 %fusion.114 = f32[2,4,16,128]{3,2,1,0:T(8,128)S(1)} fusion(s32[16384,2]{0,1:T(2,128)S(1)} %get-tuple-element.170, bf16[4,16384,2,16]{1,3,0,2:T(8,128)(2,1)S(1)} %fusion.113), kind=kOutput, calls=%fused_computation.8.clone.3 | convolution fusion | flops 541065216 | bytes 4390912 | tf_op jit(solution)/shard_map/while/body/eval_jaxpr/tpoh,pol->othl/dot_general | solution.py:66
  204.7 4.9 %fusion.114 = f32[2,4,16,128]{3,2,1,0:T(8,128)S(1)} fusion(s32[16384,2]{0,1:T(2,128)S(1)} %get-tuple-element.170, bf16[4,16384,2,16]{1,3,0,2:T(8,128)(2,1)S(1)} %fusion.113), kind=kOutput, calls=%fused_computation.8.clone.3 | convolution fusion | flops 541065216 | bytes 4390912 | tf_op jit(solution)/shard_map/while/body/eval_jaxpr/tpoh,pol->othl/dot_general | solution.py:66
  212.5 4.9 %fusion.114 = f32[2,4,16,128]{3,2,1,0:T(8,128)S(1)} fusion(s32[16384,2]{0,1:T(2,128)S(1)} %get-tuple-element.170, bf16[4,16384,2,16]{1,3,0,2:T(8,128)(2,1)S(1)} %fusion.113), kind=kOutput, calls=%fused_computation.8.clone.3 | convolution fusion | flops 541065216 | bytes 4390912 | tf_op jit(solution)/shard_map/while/body/eval_jaxpr/tpoh,pol->othl/dot_general | solution.py:66
  220.4 4.9 %fusion.114 = f32[2,4,16,128]{3,2,1,0:T(8,128)S(1)} fusion(s32[16384,2]{0,1:T(2,128)S(1)} %get-tuple-element.170, bf16[4,16384,2,16]{1,3,0,2:T(8,128)(2,1)S(1)} %fusion.113), kind=kOutput, calls=%fused_computation.8.clone.3 | convolution fusion | flops 541065216 | bytes 4390912 | tf_op jit(solution)/shard_map/while/body/eval_jaxpr/tpoh,pol->othl/dot_general | solution.py:66
  228.2 4.9 %fusion.114 = f32[2,4,16,128]{3,2,1,0:T(8,128)S(1)} fusion(s32[16384,2]{0,1:T(2,128)S(1)} %get-tuple-element.170, bf16[4,16384,2,16]{1,3,0,2:T(8,128)(2,1)S(1)} %fusion.113), kind=kOutput, calls=%fused_computation.8.clone.3 | convolution fusion | flops 541065216 | bytes 4390912 | tf_op jit(solution)/shard_map/while/body/eval_jaxpr/tpoh,pol->othl/dot_general | solution.py:66
  236.1 4.9 %fusion.114 = f32[2,4,16,128]{3,2,1,0:T(8,128)S(1)} fusion(s32[16384,2]{0,1:T(2,128)S(1)} %get-tuple-element.170, bf16[4,16384,2,16]{1,3,0,2:T(8,128)(2,1)S(1)} %fusion.113), kind=kOutput, calls=%fused_computation.8.clone.3 | convolution fusion | flops 541065216 | bytes 4390912 | tf_op jit(solution)/shard_map/while/body/eval_jaxpr/tpoh,pol->othl/dot_general | solution.py:66
  243.9 4.9 %fusion.114 = f32[2,4,16,128]{3,2,1,0:T(8,128)S(1)} fusion(s32[16384,2]{0,1:T(2,128)S(1)} %get-tuple-element.170, bf16[4,16384,2,16]{1,3,0,2:T(8,128)(2,1)S(1)} %fusion.113), kind=kOutput, calls=%fused_computation.8.clone.3 | convolution fusion | flops 541065216 | bytes 4390912 | tf_op jit(solution)/shard_map/while/body/eval_jaxpr/tpoh,pol->othl/dot_general | solution.py:66
  251.8 4.9 %fusion.114 = f32[2,4,16,128]{3,2,1,0:T(8,128)S(1)} fusion(s32[16384,2]{0,1:T(2,128)S(1)} %get-tuple-element.170, bf16[4,16384,2,16]{1,3,0,2:T(8,128)(2,1)S(1)} %fusion.113), kind=kOutput, calls=%fused_computation.8.clone.3 | convolution fusion | flops 541065216 | bytes 4390912 | tf_op jit(solution)/shard_map/while/body/eval_jaxpr/tpoh,pol->othl/dot_general | solution.py:66
  259.7 4.9 %fusion.114 = f32[2,4,16,128]{3,2,1,0:T(8,128)S(1)} fusion(s32[16384,2]{0,1:T(2,128)S(1)} %get-tuple-element.170, bf16[4,16384,2,16]{1,3,0,2:T(8,128)(2,1)S(1)} %fusion.113), kind=kOutput, calls=%fused_computation.8.clone.3 | convolution fusion | flops 541065216 | bytes 4390912 | tf_op jit(solution)/shard_map/while/body/eval_jaxpr/tpoh,pol->othl/dot_general | solution.py:66
  267.5 4.9 %fusion.114 = f32[2,4,16,128]{3,2,1,0:T(8,128)S(1)} fusion(s32[16384,2]{0,1:T(2,128)S(1)} %get-tuple-element.170, bf16[4,16384,2,16]{1,3,0,2:T(8,128)(2,1)S(1)} %fusion.113), kind=kOutput, calls=%fused_computation.8.clone.3 | convolution fusion | flops 541065216 | bytes 4390912 | tf_op jit(solution)/shard_map/while/body/eval_jaxpr/tpoh,pol->othl/dot_general | solution.py:66
  275.4 4.9 %fusion.114 = f32[2,4,16,128]{3,2,1,0:T(8,128)S(1)} fusion(s32[16384,2]{0,1:T(2,128)S(1)} %get-tuple-element.170, bf16[4,16384,2,16]{1,3,0,2:T(8,128)(2,1)S(1)} %fusion.113), kind=kOutput, calls=%fused_computation.8.clone.3 | convolution fusion | flops 541065216 | bytes 4390912 | tf_op jit(solution)/shard_map/while/body/eval_jaxpr/tpoh,pol->othl/dot_general | solution.py:66
  283.2 4.9 %fusion.114 = f32[2,4,16,128]{3,2,1,0:T(8,128)S(1)} fusion(s32[16384,2]{0,1:T(2,128)S(1)} %get-tuple-element.170, bf16[4,16384,2,16]{1,3,0,2:T(8,128)(2,1)S(1)} %fusion.113), kind=kOutput, calls=%fused_computation.8.clone.3 | convolution fusion | flops 541065216 | bytes 4390912 | tf_op jit(solution)/shard_map/while/body/eval_jaxpr/tpoh,pol->othl/dot_general | solution.py:66
  291.1 4.9 %fusion.114 = f32[2,4,16,128]{3,2,1,0:T(8,128)S(1)} fusion(s32[16384,2]{0,1:T(2,128)S(1)} %get-tuple-element.170, bf16[4,16384,2,16]{1,3,0,2:T(8,128)(2,1)S(1)} %fusion.113), kind=kOutput, calls=%fused_computation.8.clone.3 | convolution fusion | flops 541065216 | bytes 4390912 | tf_op jit(solution)/shard_map/while/body/eval_jaxpr/tpoh,pol->othl/dot_general | solution.py:66
  296.6 13.7 %all_to_all.51 = f32[32,16,128]{2,0,1:T(8,128)S(1)} all-to-all(f32[32,16,128]{2,0,1:T(8,128)S(1)} %copy.30), channel_id=1, replica_groups=mesh['box'=16,'panel'=8] {'box'}, dimensions={1} | all-to-all | bytes 524288 | tf_op jit(solution)/shard_map/all_to_all | solution.py:90
  (282 shorter events, 62.8 us)
Async XLA Ops:
  0.6 24.7 %copy-start.7 = (f32[256,512]{1,0:T(8,128)S(1)}, f32[256,512]{1,0:T(8,128)}, u32[]{:S(2)}) copy-start(f32[256,512]{1,0:T(8,128)} %param.8) | copy-start | bytes 1572868
  0.6 24.7 %copy-start = (f32[256,512]{1,0:T(8,128)S(1)}, f32[256,512]{1,0:T(8,128)}, u32[]{:S(2)}) copy-start(f32[256,512]{1,0:T(8,128)} %param.10) | copy-start | bytes 1572868
  0.7 24.7 %copy-start.1 = (s32[256,512]{1,0:T(8,128)S(1)}, s32[256,512]{1,0:T(8,128)}, u32[]{:S(2)}) copy-start(s32[256,512]{1,0:T(8,128)} %param.9) | copy-start | bytes 1572868
  1.5 23.8 %collective-permute-start = (f32[1,512]{1,0:T(1,128)S(1)}, f32[1,512]{1,0:T(1,128)S(1)}, u32[]{:S(2)}, u32[]{:S(2)}) collective-permute-start(f32[1,512]{1,0:T(1,128)S(1)} %get-tuple-element.135), channel_id=1, source_target_pairs={{8,0},{16,8},{24,16},{32,24},{40,32},{48,40},{56,48},{64,56},{72,6... | collective-permute-start | bytes 6152 | tf_op jit(solution)/shard_map/ppermute | solution.py:20
  2.8 22.6 %collective-permute-start.1 = (f32[1,512]{1,0:T(1,128)S(1)}, f32[1,512]{1,0:T(1,128)S(1)}, u32[]{:S(2)}, u32[]{:S(2)}) collective-permute-start(f32[1,512]{1,0:T(1,128)S(1)} %get-tuple-element.136), channel_id=1, source_target_pairs={{0,8},{8,16},{16,24},{24,32},{32,40},{40,48},{48,56},{56,64},{64,7... | collective-permute-start | bytes 6152 | tf_op jit(solution)/shard_map/ppermute | solution.py:19
  8.4 16.9 %collective-permute-start.2 = (f32[256,1]{1,0:T(8,128)S(1)}, f32[256,1]{1,0:T(8,128)S(1)}, u32[]{:S(2)}, u32[]{:S(2)}) collective-permute-start(f32[256,1]{1,0:T(8,128)S(1)} %get-tuple-element.134), channel_id=1, source_target_pairs={{1,0},{2,1},{3,2},{4,3},{5,4},{6,5},{7,6},{9,8},{10,9},{11,10},{12... | collective-permute-start | bytes 3080 | tf_op jit(solution)/shard_map/ppermute | solution.py:20
  9.7 15.6 %collective-permute-start.3 = (f32[256,1]{1,0:T(8,128)S(1)}, f32[256,1]{1,0:T(8,128)S(1)}, u32[]{:S(2)}, u32[]{:S(2)}) collective-permute-start(f32[256,1]{1,0:T(8,128)S(1)} %get-tuple-element.133), channel_id=1, source_target_pairs={{0,1},{1,2},{2,3},{3,4},{4,5},{5,6},{6,7},{8,9},{9,10},{10,11},{11... | collective-permute-start | bytes 3080 | tf_op jit(solution)/shard_map/ppermute | solution.py:19
  15.1 32.0 %all-to-all-start.1 = ((bf16[1024,16,32]{0,2,1:T(8,128)(2,1)}), bf16[1024,16,32]{0,2,1:T(8,128)(2,1)S(1)}, u32[]{:S(2)}, u32[]{:S(2)}) async-start(bf16[1024,16,32]{0,2,1:T(8,128)(2,1)} %bitcast.105), calls=%async_computation.1 | async-start | bytes 2097152 | tf_op jit(solution)/shard_map/all_to_all | solution.py:87
  26.2 20.9 %copy-start.2 = (f32[256,512]{1,0:T(8,128)}, f32[256,512]{1,0:T(8,128)S(1)}, u32[]{:S(2)}) copy-start(f32[256,512]{1,0:T(8,128)S(1)} %fusion.80) | copy-start | bytes 1572868
  26.2 13.2 %collective-permute-start.4 = (f32[1,512]{1,0:T(1,128)S(1)}, f32[1,512]{1,0:T(1,128)S(1)}, u32[]{:S(2)}, u32[]{:S(2)}) collective-permute-start(f32[1,512]{1,0:T(1,128)S(1)} %get-tuple-element.131), channel_id=1, source_target_pairs={{8,0},{16,8},{24,16},{32,24},{40,32},{48,40},{56,48},{64,56},{72,6... | collective-permute-start | bytes 6152 | tf_op jit(solution)/shard_map/ppermute | solution.py:20
  27.5 12.0 %collective-permute-start.5 = (f32[1,512]{1,0:T(1,128)S(1)}, f32[1,512]{1,0:T(1,128)S(1)}, u32[]{:S(2)}, u32[]{:S(2)}) collective-permute-start(f32[1,512]{1,0:T(1,128)S(1)} %get-tuple-element.132), channel_id=1, source_target_pairs={{0,8},{8,16},{16,24},{24,32},{32,40},{40,48},{48,56},{56,64},{64,7... | collective-permute-start | bytes 6152 | tf_op jit(solution)/shard_map/ppermute | solution.py:19
  32.2 7.3 %collective-permute-start.6 = (f32[256,1]{1,0:T(8,128)S(1)}, f32[256,1]{1,0:T(8,128)S(1)}, u32[]{:S(2)}, u32[]{:S(2)}) collective-permute-start(f32[256,1]{1,0:T(8,128)S(1)} %get-tuple-element.130), channel_id=1, source_target_pairs={{1,0},{2,1},{3,2},{4,3},{5,4},{6,5},{7,6},{9,8},{10,9},{11,10},{12... | collective-permute-start | bytes 3080 | tf_op jit(solution)/shard_map/ppermute | solution.py:20
  33.5 6.0 %collective-permute-start.7 = (f32[256,1]{1,0:T(8,128)S(1)}, f32[256,1]{1,0:T(8,128)S(1)}, u32[]{:S(2)}, u32[]{:S(2)}) collective-permute-start(f32[256,1]{1,0:T(8,128)S(1)} %get-tuple-element.129), channel_id=1, source_target_pairs={{0,1},{1,2},{2,3},{3,4},{4,5},{5,6},{6,7},{8,9},{9,10},{10,11},{11... | collective-permute-start | bytes 3080 | tf_op jit(solution)/shard_map/ppermute | solution.py:19
  39.4 24.0 %copy-start.8 = (s32[128]{0:T(128)S(1)}, s32[128]{0:T(128)}, u32[]{:S(2)}) copy-start(s32[128]{0:T(128)} %param.11) | copy-start | bytes 1540
  40.2 0.8 copy-start.3
  41.7 21.7 %collective-permute-start.10 = (f32[256,1]{1,0:T(8,128)}, f32[256,1]{1,0:T(8,128)S(1)}, u32[]{:S(2)}, u32[]{:S(2)}) collective-permute-start(f32[256,1]{1,0:T(8,128)} %get-tuple-element.126), channel_id=1, source_target_pairs={{1,0},{2,1},{3,2},{4,3},{5,4},{6,5},{7,6},{9,8},{10,9},{11,10},{12... | collective-permute-start | bytes 3080 | tf_op jit(solution)/shard_map/ppermute | solution.py:20
  43.0 20.4 %collective-permute-start.11 = (f32[256,1]{1,0:T(8,128)S(1)}, f32[256,1]{1,0:T(8,128)S(1)}, u32[]{:S(2)}, u32[]{:S(2)}) collective-permute-start(f32[256,1]{1,0:T(8,128)S(1)} %get-tuple-element.125), channel_id=1, source_target_pairs={{0,1},{1,2},{2,3},{3,4},{4,5},{5,6},{6,7},{8,9},{9,10},{10,11},{11... | collective-permute-start | bytes 3080 | tf_op jit(solution)/shard_map/ppermute | solution.py:19
  47.1 1.0 copy-start.5
  48.0 116.9 %all-to-all-start = ((s32[1024,16,32]{0,2,1:T(8,128)}), s32[1024,16,32]{0,2,1:T(8,128)S(1)}, u32[]{:S(2)}, u32[]{:S(2)}) async-start(s32[1024,16,32]{0,2,1:T(8,128)} %bitcast), calls=%async_computation | async-start | bytes 4194304 | tf_op jit(solution)/shard_map/all_to_all | solution.py:88
  57.6 11.6 %collective-permute-start.8 = (f32[1,512]{1,0:T(1,128)S(1)}, f32[1,512]{1,0:T(1,128)S(1)}, u32[]{:S(2)}, u32[]{:S(2)}) collective-permute-start(f32[1,512]{1,0:T(1,128)S(1)} %get-tuple-element.127), channel_id=1, source_target_pairs={{8,0},{16,8},{24,16},{32,24},{40,32},{48,40},{56,48},{64,56},{72,6... | collective-permute-start | bytes 6152 | tf_op jit(solution)/shard_map/ppermute | solution.py:20
  58.8 10.4 %collective-permute-start.9 = (f32[1,512]{1,0:T(1,128)S(1)}, f32[1,512]{1,0:T(1,128)S(1)}, u32[]{:S(2)}, u32[]{:S(2)}) collective-permute-start(f32[1,512]{1,0:T(1,128)S(1)} %get-tuple-element.128), channel_id=1, source_target_pairs={{0,8},{8,16},{16,24},{24,32},{32,40},{40,48},{48,56},{56,64},{64,7... | collective-permute-start | bytes 6152 | tf_op jit(solution)/shard_map/ppermute | solution.py:19
  71.9 13.3 %copy-start.4 = (f32[256,512]{1,0:T(8,128)}, f32[256,512]{1,0:T(8,128)S(1)}, u32[]{:S(2)}) copy-start(f32[256,512]{1,0:T(8,128)S(1)} %fusion.44) | copy-start | bytes 1572868
  72.8 32.5 %collective-permute-start.14 = (f32[256,1]{1,0:T(8,128)}, f32[256,1]{1,0:T(8,128)S(1)}, u32[]{:S(2)}, u32[]{:S(2)}) collective-permute-start(f32[256,1]{1,0:T(8,128)} %get-tuple-element.122), channel_id=1, source_target_pairs={{1,0},{2,1},{3,2},{4,3},{5,4},{6,5},{7,6},{9,8},{10,9},{11,10},{12... | collective-permute-start | bytes 3080 | tf_op jit(solution)/shard_map/ppermute | solution.py:20
  74.1 31.2 %collective-permute-start.15 = (f32[256,1]{1,0:T(8,128)}, f32[256,1]{1,0:T(8,128)}, u32[]{:S(2)}, u32[]{:S(2)}) collective-permute-start(f32[256,1]{1,0:T(8,128)} %get-tuple-element.121), channel_id=1, source_target_pairs={{0,1},{1,2},{2,3},{3,4},{4,5},{5,6},{6,7},{8,9},{9,10},{10,11},{11... | collective-permute-start | bytes 3080 | tf_op jit(solution)/shard_map/ppermute | solution.py:19
  85.8 19.5 %collective-permute-start.12 = (f32[1,512]{1,0:T(1,128)}, f32[1,512]{1,0:T(1,128)S(1)}, u32[]{:S(2)}, u32[]{:S(2)}) collective-permute-start(f32[1,512]{1,0:T(1,128)} %get-tuple-element.123), channel_id=1, source_target_pairs={{8,0},{16,8},{24,16},{32,24},{40,32},{48,40},{56,48},{64,56},{72,6... | collective-permute-start | bytes 6152 | tf_op jit(solution)/shard_map/ppermute | solution.py:20
  87.0 18.2 %collective-permute-start.13 = (f32[1,512]{1,0:T(1,128)S(1)}, f32[1,512]{1,0:T(1,128)S(1)}, u32[]{:S(2)}, u32[]{:S(2)}) collective-permute-start(f32[1,512]{1,0:T(1,128)S(1)} %get-tuple-element.124), channel_id=1, source_target_pairs={{0,8},{8,16},{16,24},{24,32},{32,40},{40,48},{48,56},{56,64},{64,7... | collective-permute-start | bytes 6152 | tf_op jit(solution)/shard_map/ppermute | solution.py:19
  108.1 0.8 copy-start.6
where the time goes:
time: 313 us; the launch traced here: 311 us
  matrix products  78.2 us (25%)
  starting transfers between devices  68.7 us (22%)
  blocking collectives  62.4 us (20%)
  other arithmetic  51.4 us (16%)
  local copies, waits for them, and re-layouts  41.6 us (13%)
  waiting for transfers between devices  5.8 us (2%)
    dot_general x16, matrix products, one_block(): jnp.einsum('tpoh,pol->othl', left, right, preferred_element_type=jnp.floa...  78.2 us
    all_gather x1, blocking collectives, on_device(): every = lax.all_gather(sample, ('box', 'panel'), axis=1, tiled=True)  48.7 us
    ppermute x8, starting transfers between devices, padded(): lax.ppermute(last, axis, up)  39.4 us
    unnamed x25, local copies, waits for them, and re-layouts  14.5 us
    mul x16, other arithmetic, one_block(): amp_rows.astype(jnp.float32)[None, :, :] * sample[:, :, None]  14.3 us
    all_to_all x1, blocking collectives, on_device(): lax.all_to_all(finished, 'box', split_axis=1, concat_axis=0, tiled=True)  13.7 us
    dot_general x16, other arithmetic, one_block(): jnp.einsum('tpoh,pol->othl', left, right, preferred_element_type=jnp.floa...  13.6 us
    ppermute x8, starting transfers between devices, padded(): lax.ppermute(initial, axis, [(b, a) for a, b in up])  10.3 us
  transfers between devices with their start and end apart: 18, of which 1 were waited for; matrix products, arithmetic and copies ran while one was open for 12% of the time, Pallas kernels for 0%

commit v1 on v0

--- a/solution.py
+++ b/solution.py
@@ -83,7 +83,8 @@
         field = advance(extended, maskf, base_visc)
         taken.append(field.reshape(-1)[panel_cell])
     sample = jnp.stack(taken)
-    every = lax.all_gather(sample, ("box", "panel"), axis=1, tiled=True)
+    sent = jnp.stack([sample] * lax.axis_size(("box", "panel")))
+    every = jnp.concatenate(lax.all_to_all(sent, ("box", "panel"), 0, 0), axis=1)
     amp_all = lax.all_to_all(amplitude, "box", split_axis=1, concat_axis=0, tiled=True)
     bin_all = lax.all_to_all(delay_bin, "box", split_axis=1, concat_axis=0, tiled=True)
     finished = signal_terms(amp_all, bin_all, every)

time: 313 us -> 300 us (0.958)
  blocking collectives: 62.4 us -> 12 us
  waiting for transfers between devices: 5.8 us -> 50.6 us
  local copies, waits for them, and re-layouts: 41.6 us -> 29.6 us
  starting transfers between devices: 68.7 us -> 74.1 us
    all_gather x1 -> x0, blocking collectives: 48.7 us -> none  [on_device(): every = lax.all_gather(sample, ('box', 'panel'), axis=1, tiled=True)]
    all_to_all x1, waiting for transfers between devices: 0.01 us -> 22.9 us  [on_device(): lax.all_to_all(delay_bin, 'box', split_axis=1, concat_axis=0, tiled=True)]
    all_to_all x0 -> x1, starting transfers between devices: none -> 18.6 us  [on_device(): lax.all_to_all(sent, ('box', 'panel'), 0, 0)]
    all_to_all x1, waiting for transfers between devices: 0.01 us -> 16.1 us  [on_device(): lax.all_to_all(amplitude, 'box', split_axis=1, concat_axis=0, tiled=True)]
    all_to_all x0 -> x1, waiting for transfers between devices: none -> 8.43 us  [on_device(): lax.all_to_all(sent, ('box', 'panel'), 0, 0)]
    unnamed x25 -> x22, local copies, waits for them, and re-layouts: 14.5 us -> 7.15 us
    all_to_all x1, starting transfers between devices: 10.3 us -> 3.65 us  [on_device(): lax.all_to_all(amplitude, 'box', split_axis=1, concat_axis=0, tiled=True)]
    ppermute x8, waiting for transfers between devices: 5.77 us -> 0.02 us  [padded(): lax.ppermute(initial, axis, [(b, a) for a, b in up])]
  transfers between devices with their start and end apart: 18 -> 19, of which waited for: 1 -> 6; matrix products, arithmetic and copies ran while one was open for 12% -> 5% of each run, Pallas kernels for 0% -> 0%
where the time goes in v1:
time: 300 us; the launch traced here: 298 us
  matrix products  78.3 us (26%)
  starting transfers between devices  74.1 us (25%)
  waiting for transfers between devices  50.6 us (17%)
  other arithmetic  50.3 us (17%)
  local copies, waits for them, and re-layouts  29.6 us (10%)
  blocking collectives  12 us (4%)
    dot_general x16, matrix products, one_block(): jnp.einsum('tpoh,pol->othl', left, right, preferred_element_type=jnp.floa...  78.3 us
    ppermute x8, starting transfers between devices, padded(): lax.ppermute(last, axis, up)  37.6 us
    all_to_all x1, waiting for transfers between devices, on_device(): lax.all_to_all(delay_bin, 'box', split_axis=1, concat_axis=0, tiled=True)  22.9 us
    all_to_all x1, starting transfers between devices, on_device(): lax.all_to_all(sent, ('box', 'panel'), 0, 0)  18.6 us
    all_to_all x1, waiting for transfers between devices, on_device(): lax.all_to_all(amplitude, 'box', split_axis=1, concat_axis=0, tiled=True)  16.1 us
    mul x16, other arithmetic, one_block(): amp_rows.astype(jnp.float32)[None, :, :] * sample[:, :, None]  14.3 us
    dot_general x16, other arithmetic, one_block(): jnp.einsum('tpoh,pol->othl', left, right, preferred_element_type=jnp.floa...  13.6 us
    all_to_all x1, blocking collectives, on_device(): lax.all_to_all(finished, 'box', split_axis=1, concat_axis=0, tiled=True)  12 us
  transfers between devices with their start and end apart: 19, of which 6 were waited for; matrix products, arithmetic and copies ran while one was open for 5% of the time, Pallas kernels for 0%

profile of v1, /device:TPU:0, one launch (start us, length us, event | category | flops | bytes accessed | tf_op | source)
XLA Modules:
  0.0 298.0 jit_solution(9250340820826021262)
XLA Ops:
  1.5 1.3 collective-permute-start
  2.8 4.6 %collective-permute-start.1 = (f32[1,512]{1,0:T(1,128)S(1)}, f32[1,512]{1,0:T(1,128)S(1)}, u32[]{:S(2)}, u32[]{:S(2)}) collective-permute-start(f32[1,512]{1,0:T(1,128)S(1)} %get-tuple-element.141), channel_id=1, source_target_pairs={{0,8},{8,16},{16,24},{24,32},{32,40},{40,48},{48,56},{56,64},{64,7... | collective-permute-start | bytes 6152 | tf_op jit(solution)/shard_map/ppermute | solution.py:19
  8.4 1.3 collective-permute-start.2
  9.7 3.0 %collective-permute-start.3 = (f32[256,1]{1,0:T(8,128)S(1)}, f32[256,1]{1,0:T(8,128)S(1)}, u32[]{:S(2)}, u32[]{:S(2)}) collective-permute-start(f32[256,1]{1,0:T(8,128)S(1)} %get-tuple-element.138), channel_id=1, source_target_pairs={{0,1},{1,2},{2,3},{3,4},{4,5},{5,6},{6,7},{8,9},{9,10},{10,11},{11... | collective-permute-start | bytes 3080 | tf_op jit(solution)/shard_map/ppermute | solution.py:19
  13.7 3.1 %fusion.80 = f32[256,512]{1,0:T(8,128)S(1)} fusion(f32[256,512]{1,0:T(8,128)} %param.8, f32[1,512]{1,0:T(1,128)S(1)} %collective-permute-done.1, f32[1,512]{1,0:T(1,128)S(1)} %collective-permute-done, f32[256,512]{1,0:T(8,128)} %param.10, f32[256,1]{1,0:T(8,128)S(1)} %collective-permute-done.2, f32[256,1]{1,0:T(8,128)S(1)} %collective-permute-done.3, ...), kind=kLoop, calls=%fused_computation.131 | loop fusion | flops 5242880 | bytes 2103296 | tf_op jit(solution)/shard_map/mul | solution.py:43
  16.9 1.3 collective-permute-start.4
  18.2 4.6 %collective-permute-start.5 = (f32[1,512]{1,0:T(1,128)S(1)}, f32[1,512]{1,0:T(1,128)S(1)}, u32[]{:S(2)}, u32[]{:S(2)}) collective-permute-start(f32[1,512]{1,0:T(1,128)S(1)} %get-tuple-element.137), channel_id=1, source_target_pairs={{0,8},{8,16},{16,24},{24,32},{32,40},{40,48},{48,56},{56,64},{64,7... | collective-permute-start | bytes 6152 | tf_op jit(solution)/shard_map/ppermute | solution.py:19
  22.8 1.3 collective-permute-start.6
  24.1 4.3 %collective-permute-start.7 = (f32[256,1]{1,0:T(8,128)S(1)}, f32[256,1]{1,0:T(8,128)S(1)}, u32[]{:S(2)}, u32[]{:S(2)}) collective-permute-start(f32[256,1]{1,0:T(8,128)S(1)} %get-tuple-element.134), channel_id=1, source_target_pairs={{0,1},{1,2},{2,3},{3,4},{4,5},{5,6},{6,7},{8,9},{9,10},{10,11},{11... | collective-permute-start | bytes 3080 | tf_op jit(solution)/shard_map/ppermute | solution.py:19
  29.4 2.0 fusion.62
  31.5 1.3 collective-permute-start.10
  32.8 6.3 %collective-permute-start.11 = (f32[256,1]{1,0:T(8,128)S(1)}, f32[256,1]{1,0:T(8,128)S(1)}, u32[]{:S(2)}, u32[]{:S(2)}) collective-permute-start(f32[256,1]{1,0:T(8,128)S(1)} %get-tuple-element.130), channel_id=1, source_target_pairs={{0,1},{1,2},{2,3},{3,4},{4,5},{5,6},{6,7},{8,9},{9,10},{10,11},{11... | collective-permute-start | bytes 3080 | tf_op jit(solution)/shard_map/ppermute | solution.py:19
  39.2 1.3 collective-permute-start.8
  40.5 4.5 %collective-permute-start.9 = (f32[1,512]{1,0:T(1,128)S(1)}, f32[1,512]{1,0:T(1,128)S(1)}, u32[]{:S(2)}, u32[]{:S(2)}) collective-permute-start(f32[1,512]{1,0:T(1,128)S(1)} %get-tuple-element.133), channel_id=1, source_target_pairs={{0,8},{8,16},{16,24},{24,32},{32,40},{40,48},{48,56},{56,64},{64,7... | collective-permute-start | bytes 6152 | tf_op jit(solution)/shard_map/ppermute | solution.py:19
  47.2 1.3 collective-permute-start.14
  48.5 4.0 %collective-permute-start.15 = (f32[256,1]{1,0:T(8,128)S(1)}, f32[256,1]{1,0:T(8,128)S(1)}, u32[]{:S(2)}, u32[]{:S(2)}) collective-permute-start(f32[256,1]{1,0:T(8,128)S(1)} %get-tuple-element.126), channel_id=1, source_target_pairs={{0,1},{1,2},{2,3},{3,4},{4,5},{5,6},{6,7},{8,9},{9,10},{10,11},{11... | collective-permute-start | bytes 3080 | tf_op jit(solution)/shard_map/ppermute | solution.py:19
  52.6 1.3 collective-permute-start.12
  53.9 6.2 %collective-permute-start.13 = (f32[1,512]{1,0:T(1,128)S(1)}, f32[1,512]{1,0:T(1,128)S(1)}, u32[]{:S(2)}, u32[]{:S(2)}) collective-permute-start(f32[1,512]{1,0:T(1,128)S(1)} %get-tuple-element.129), channel_id=1, source_target_pairs={{0,8},{8,16},{16,24},{24,32},{32,40},{40,48},{48,56},{56,64},{64,7... | collective-permute-start | bytes 6152 | tf_op jit(solution)/shard_map/ppermute | solution.py:19
  67.6 18.6 %all-to-all-start.2 = ((f32[128,4,128]{2,1,0:T(4,128)}), f32[128,4,128]{2,1,0:T(4,128)S(1)}, u32[]{:S(2)}, u32[]{:S(2)}) async-start(f32[128,4,128]{2,1,0:T(4,128)} %stack.17), calls=%async_computation.2 | async-start | bytes 524288 | tf_op jit(solution)/shard_map/all_to_all | solution.py:87
  86.3 2.3 copy.37
  88.5 8.4 %all-to-all-done.2 = f32[128,4,128]{2,1,0:T(4,128)S(1)} async-done(((f32[128,4,128]{2,1,0:T(4,128)}), f32[128,4,128]{2,1,0:T(4,128)S(1)}, u32[]{:S(2)}, u32[]{:S(2)}) %all-to-all-start.2) | async-done | bytes 262176 | tf_op jit(solution)/shard_map/all_to_all | solution.py:87
  97.0 3.7 %all-to-all-start.1 = ((bf16[1024,16,32]{0,2,1:T(8,128)(2,1)}), bf16[1024,16,32]{0,2,1:T(8,128)(2,1)S(1)}, u32[]{:S(2)}, u32[]{:S(2)}) async-start(bf16[1024,16,32]{0,2,1:T(8,128)(2,1)} %bitcast.3), calls=%async_computation.1 | async-start | bytes 2097152 | tf_op jit(solution)/shard_map/all_to_all | solution.py:88
  100.6 1.9 copy.35
  102.5 16.1 %all-to-all-done.1 = bf16[1024,16,32]{0,2,1:T(8,128)(2,1)S(1)} async-done(((bf16[1024,16,32]{0,2,1:T(8,128)(2,1)}), bf16[1024,16,32]{0,2,1:T(8,128)(2,1)S(1)}, u32[]{:S(2)}, u32[]{:S(2)}) %all-to-all-start.1) | async-done | bytes 1048608 | tf_op jit(solution)/shard_map/all_to_all | solution.py:88
  118.6 3.9 %all-to-all-start = ((s32[1024,16,32]{0,2,1:T(8,128)}), s32[1024,16,32]{0,2,1:T(8,128)S(1)}, u32[]{:S(2)}, u32[]{:S(2)}) async-start(s32[1024,16,32]{0,2,1:T(8,128)} %bitcast), calls=%async_computation | async-start | bytes 4194304 | tf_op jit(solution)/shard_map/all_to_all | solution.py:89
  123.5 1.6 copy.38
  125.0 2.6 reshape.103
  127.7 22.9 %all-to-all-done = s32[1024,16,32]{0,2,1:T(8,128)S(1)} async-done(((s32[1024,16,32]{0,2,1:T(8,128)}), s32[1024,16,32]{0,2,1:T(8,128)S(1)}, u32[]{:S(2)}, u32[]{:S(2)}) %all-to-all-start) | async-done | bytes 2097184 | tf_op jit(solution)/shard_map/all_to_all | solution.py:89
  150.6 2.6 copy.36
  153.2 3.1 %reshape.102 = s32[16384,16,2]{0,2,1:T(2,128)S(1)} reshape(s32[16,1024,32]{1,0,2:T(8,128)} %copy.36) | data formatting | bytes 4194304 | tf_op jit(solution)/shard_map/reshape | solution.py:52
  156.3 128.7 %while.13 = (s32[]{:T(128)}, f32[16,2,2048]{2,1,0:T(2,128)S(1)}, s32[16,16384,2]{1,2,0:T(2,128)S(1)}, bf16[16,16384,2]{1,2,0:T(2,128)(2,1)}, f32[4,128,128]{2,1,0:T(8,128)S(1)}, /*index=5*/s32[]{:T(128)}) while((s32[]{:T(128)}, f32[16,2,2048]{2,1,0:T(2,128)S(1)}, s32[16,16384,2]{1,2,0:T(2,128)S(1)}, ...), condition=%wide.region_1.2_spmd.clone, body=%wide.region_0.1_spmd.clone.sunk | while | flops 544616448 | bytes 12238737 | solution.py:73
  159.1 4.9 %fusion.114 = f32[2,4,16,128]{3,2,1,0:T(8,128)S(1)} fusion(s32[16384,2]{0,1:T(2,128)S(1)} %get-tuple-element.175, bf16[4,16384,2,16]{1,3,0,2:T(8,128)(2,1)S(1)} %fusion.113), kind=kOutput, calls=%fused_computation.8.clone.3 | convolution fusion | flops 541065216 | bytes 4390912 | tf_op jit(solution)/shard_map/while/body/eval_jaxpr/tpoh,pol->othl/dot_general | solution.py:66
  167.1 4.9 %fusion.114 = f32[2,4,16,128]{3,2,1,0:T(8,128)S(1)} fusion(s32[16384,2]{0,1:T(2,128)S(1)} %get-tuple-element.175, bf16[4,16384,2,16]{1,3,0,2:T(8,128)(2,1)S(1)} %fusion.113), kind=kOutput, calls=%fused_computation.8.clone.3 | convolution fusion | flops 541065216 | bytes 4390912 | tf_op jit(solution)/shard_map/while/body/eval_jaxpr/tpoh,pol->othl/dot_general | solution.py:66
  175.2 4.9 %fusion.114 = f32[2,4,16,128]{3,2,1,0:T(8,128)S(1)} fusion(s32[16384,2]{0,1:T(2,128)S(1)} %get-tuple-element.175, bf16[4,16384,2,16]{1,3,0,2:T(8,128)(2,1)S(1)} %fusion.113), kind=kOutput, calls=%fused_computation.8.clone.3 | convolution fusion | flops 541065216 | bytes 4390912 | tf_op jit(solution)/shard_map/while/body/eval_jaxpr/tpoh,pol->othl/dot_general | solution.py:66
  183.2 4.9 %fusion.114 = f32[2,4,16,128]{3,2,1,0:T(8,128)S(1)} fusion(s32[16384,2]{0,1:T(2,128)S(1)} %get-tuple-element.175, bf16[4,16384,2,16]{1,3,0,2:T(8,128)(2,1)S(1)} %fusion.113), kind=kOutput, calls=%fused_computation.8.clone.3 | convolution fusion | flops 541065216 | bytes 4390912 | tf_op jit(solution)/shard_map/while/body/eval_jaxpr/tpoh,pol->othl/dot_general | solution.py:66
  191.2 4.9 %fusion.114 = f32[2,4,16,128]{3,2,1,0:T(8,128)S(1)} fusion(s32[16384,2]{0,1:T(2,128)S(1)} %get-tuple-element.175, bf16[4,16384,2,16]{1,3,0,2:T(8,128)(2,1)S(1)} %fusion.113), kind=kOutput, calls=%fused_computation.8.clone.3 | convolution fusion | flops 541065216 | bytes 4390912 | tf_op jit(solution)/shard_map/while/body/eval_jaxpr/tpoh,pol->othl/dot_general | solution.py:66
  199.3 4.9 %fusion.114 = f32[2,4,16,128]{3,2,1,0:T(8,128)S(1)} fusion(s32[16384,2]{0,1:T(2,128)S(1)} %get-tuple-element.175, bf16[4,16384,2,16]{1,3,0,2:T(8,128)(2,1)S(1)} %fusion.113), kind=kOutput, calls=%fused_computation.8.clone.3 | convolution fusion | flops 541065216 | bytes 4390912 | tf_op jit(solution)/shard_map/while/body/eval_jaxpr/tpoh,pol->othl/dot_general | solution.py:66
  207.3 4.9 %fusion.114 = f32[2,4,16,128]{3,2,1,0:T(8,128)S(1)} fusion(s32[16384,2]{0,1:T(2,128)S(1)} %get-tuple-element.175, bf16[4,16384,2,16]{1,3,0,2:T(8,128)(2,1)S(1)} %fusion.113), kind=kOutput, calls=%fused_computation.8.clone.3 | convolution fusion | flops 541065216 | bytes 4390912 | tf_op jit(solution)/shard_map/while/body/eval_jaxpr/tpoh,pol->othl/dot_general | solution.py:66
  215.4 4.9 %fusion.114 = f32[2,4,16,128]{3,2,1,0:T(8,128)S(1)} fusion(s32[16384,2]{0,1:T(2,128)S(1)} %get-tuple-element.175, bf16[4,16384,2,16]{1,3,0,2:T(8,128)(2,1)S(1)} %fusion.113), kind=kOutput, calls=%fused_computation.8.clone.3 | convolution fusion | flops 541065216 | bytes 4390912 | tf_op jit(solution)/shard_map/while/body/eval_jaxpr/tpoh,pol->othl/dot_general | solution.py:66
  223.4 4.9 %fusion.114 = f32[2,4,16,128]{3,2,1,0:T(8,128)S(1)} fusion(s32[16384,2]{0,1:T(2,128)S(1)} %get-tuple-element.175, bf16[4,16384,2,16]{1,3,0,2:T(8,128)(2,1)S(1)} %fusion.113), kind=kOutput, calls=%fused_computation.8.clone.3 | convolution fusion | flops 541065216 | bytes 4390912 | tf_op jit(solution)/shard_map/while/body/eval_jaxpr/tpoh,pol->othl/dot_general | solution.py:66
  231.5 4.9 %fusion.114 = f32[2,4,16,128]{3,2,1,0:T(8,128)S(1)} fusion(s32[16384,2]{0,1:T(2,128)S(1)} %get-tuple-element.175, bf16[4,16384,2,16]{1,3,0,2:T(8,128)(2,1)S(1)} %fusion.113), kind=kOutput, calls=%fused_computation.8.clone.3 | convolution fusion | flops 541065216 | bytes 4390912 | tf_op jit(solution)/shard_map/while/body/eval_jaxpr/tpoh,pol->othl/dot_general | solution.py:66
  239.5 4.9 %fusion.114 = f32[2,4,16,128]{3,2,1,0:T(8,128)S(1)} fusion(s32[16384,2]{0,1:T(2,128)S(1)} %get-tuple-element.175, bf16[4,16384,2,16]{1,3,0,2:T(8,128)(2,1)S(1)} %fusion.113), kind=kOutput, calls=%fused_computation.8.clone.3 | convolution fusion | flops 541065216 | bytes 4390912 | tf_op jit(solution)/shard_map/while/body/eval_jaxpr/tpoh,pol->othl/dot_general | solution.py:66
  247.5 4.9 %fusion.114 = f32[2,4,16,128]{3,2,1,0:T(8,128)S(1)} fusion(s32[16384,2]{0,1:T(2,128)S(1)} %get-tuple-element.175, bf16[4,16384,2,16]{1,3,0,2:T(8,128)(2,1)S(1)} %fusion.113), kind=kOutput, calls=%fused_computation.8.clone.3 | convolution fusion | flops 541065216 | bytes 4390912 | tf_op jit(solution)/shard_map/while/body/eval_jaxpr/tpoh,pol->othl/dot_general | solution.py:66
  255.6 4.9 %fusion.114 = f32[2,4,16,128]{3,2,1,0:T(8,128)S(1)} fusion(s32[16384,2]{0,1:T(2,128)S(1)} %get-tuple-element.175, bf16[4,16384,2,16]{1,3,0,2:T(8,128)(2,1)S(1)} %fusion.113), kind=kOutput, calls=%fused_computation.8.clone.3 | convolution fusion | flops 541065216 | bytes 4390912 | tf_op jit(solution)/shard_map/while/body/eval_jaxpr/tpoh,pol->othl/dot_general | solution.py:66
  263.6 4.9 %fusion.114 = f32[2,4,16,128]{3,2,1,0:T(8,128)S(1)} fusion(s32[16384,2]{0,1:T(2,128)S(1)} %get-tuple-element.175, bf16[4,16384,2,16]{1,3,0,2:T(8,128)(2,1)S(1)} %fusion.113), kind=kOutput, calls=%fused_computation.8.clone.3 | convolution fusion | flops 541065216 | bytes 4390912 | tf_op jit(solution)/shard_map/while/body/eval_jaxpr/tpoh,pol->othl/dot_general | solution.py:66
  271.7 4.9 %fusion.114 = f32[2,4,16,128]{3,2,1,0:T(8,128)S(1)} fusion(s32[16384,2]{0,1:T(2,128)S(1)} %get-tuple-element.175, bf16[4,16384,2,16]{1,3,0,2:T(8,128)(2,1)S(1)} %fusion.113), kind=kOutput, calls=%fused_computation.8.clone.3 | convolution fusion | flops 541065216 | bytes 4390912 | tf_op jit(solution)/shard_map/while/body/eval_jaxpr/tpoh,pol->othl/dot_general | solution.py:66
  279.7 4.9 %fusion.114 = f32[2,4,16,128]{3,2,1,0:T(8,128)S(1)} fusion(s32[16384,2]{0,1:T(2,128)S(1)} %get-tuple-element.175, bf16[4,16384,2,16]{1,3,0,2:T(8,128)(2,1)S(1)} %fusion.113), kind=kOutput, calls=%fused_computation.8.clone.3 | convolution fusion | flops 541065216 | bytes 4390912 | tf_op jit(solution)/shard_map/while/body/eval_jaxpr/tpoh,pol->othl/dot_general | solution.py:66
  285.2 12.0 %all_to_all.56 = f32[32,16,128]{2,0,1:T(8,128)S(1)} all-to-all(f32[32,16,128]{2,0,1:T(8,128)S(1)} %copy.40), channel_id=1, replica_groups=mesh['box'=16,'panel'=8] {'box'}, dimensions={1} | all-to-all | bytes 524288 | tf_op jit(solution)/shard_map/all_to_all | solution.py:91
  (297 shorter events, 64.0 us)
Async XLA Ops:
  0.6 45.7 %copy-start = (f32[256,512]{1,0:T(8,128)S(1)}, f32[256,512]{1,0:T(8,128)}, u32[]{:S(2)}) copy-start(f32[256,512]{1,0:T(8,128)} %param.10) | copy-start | bytes 1572868
  0.6 45.7 %copy-start.1 = (s32[256,512]{1,0:T(8,128)S(1)}, s32[256,512]{1,0:T(8,128)}, u32[]{:S(2)}) copy-start(s32[256,512]{1,0:T(8,128)} %param.9) | copy-start | bytes 1572868
  0.7 44.4 %copy-start.6 = (s32[128]{0:T(128)S(1)}, s32[128]{0:T(128)}, u32[]{:S(2)}) copy-start(s32[128]{0:T(128)} %param.11) | copy-start | bytes 1540
  1.5 12.2 %collective-permute-start = (f32[1,512]{1,0:T(1,128)S(1)}, f32[1,512]{1,0:T(1,128)S(1)}, u32[]{:S(2)}, u32[]{:S(2)}) collective-permute-start(f32[1,512]{1,0:T(1,128)S(1)} %get-tuple-element.140), channel_id=1, source_target_pairs={{8,0},{16,8},{24,16},{32,24},{40,32},{48,40},{56,48},{64,56},{72,6... | collective-permute-start | bytes 6152 | tf_op jit(solution)/shard_map/ppermute | solution.py:20
  2.8 11.0 %collective-permute-start.1 = (f32[1,512]{1,0:T(1,128)S(1)}, f32[1,512]{1,0:T(1,128)S(1)}, u32[]{:S(2)}, u32[]{:S(2)}) collective-permute-start(f32[1,512]{1,0:T(1,128)S(1)} %get-tuple-element.141), channel_id=1, source_target_pairs={{0,8},{8,16},{16,24},{24,32},{32,40},{40,48},{48,56},{56,64},{64,7... | collective-permute-start | bytes 6152 | tf_op jit(solution)/shard_map/ppermute | solution.py:19
  8.4 4.3 %collective-permute-start.2 = (f32[256,1]{1,0:T(8,128)S(1)}, f32[256,1]{1,0:T(8,128)S(1)}, u32[]{:S(2)}, u32[]{:S(2)}) collective-permute-start(f32[256,1]{1,0:T(8,128)S(1)} %get-tuple-element.139), channel_id=1, source_target_pairs={{1,0},{2,1},{3,2},{4,3},{5,4},{6,5},{7,6},{9,8},{10,9},{11,10},{12... | collective-permute-start | bytes 3080 | tf_op jit(solution)/shard_map/ppermute | solution.py:20
  9.7 4.0 %collective-permute-start.3 = (f32[256,1]{1,0:T(8,128)S(1)}, f32[256,1]{1,0:T(8,128)S(1)}, u32[]{:S(2)}, u32[]{:S(2)}) collective-permute-start(f32[256,1]{1,0:T(8,128)S(1)} %get-tuple-element.138), channel_id=1, source_target_pairs={{0,1},{1,2},{2,3},{3,4},{4,5},{5,6},{6,7},{8,9},{9,10},{10,11},{11... | collective-permute-start | bytes 3080 | tf_op jit(solution)/shard_map/ppermute | solution.py:19
  16.9 12.6 %collective-permute-start.4 = (f32[1,512]{1,0:T(1,128)S(1)}, f32[1,512]{1,0:T(1,128)S(1)}, u32[]{:S(2)}, u32[]{:S(2)}) collective-permute-start(f32[1,512]{1,0:T(1,128)S(1)} %get-tuple-element.136), channel_id=1, source_target_pairs={{8,0},{16,8},{24,16},{32,24},{40,32},{48,40},{56,48},{64,56},{72,6... | collective-permute-start | bytes 6152 | tf_op jit(solution)/shard_map/ppermute | solution.py:20
  18.2 11.3 %collective-permute-start.5 = (f32[1,512]{1,0:T(1,128)S(1)}, f32[1,512]{1,0:T(1,128)S(1)}, u32[]{:S(2)}, u32[]{:S(2)}) collective-permute-start(f32[1,512]{1,0:T(1,128)S(1)} %get-tuple-element.137), channel_id=1, source_target_pairs={{0,8},{8,16},{16,24},{24,32},{32,40},{40,48},{48,56},{56,64},{64,7... | collective-permute-start | bytes 6152 | tf_op jit(solution)/shard_map/ppermute | solution.py:19
  22.8 5.6 %collective-permute-start.6 = (f32[256,1]{1,0:T(8,128)S(1)}, f32[256,1]{1,0:T(8,128)S(1)}, u32[]{:S(2)}, u32[]{:S(2)}) collective-permute-start(f32[256,1]{1,0:T(8,128)S(1)} %get-tuple-element.135), channel_id=1, source_target_pairs={{1,0},{2,1},{3,2},{4,3},{5,4},{6,5},{7,6},{9,8},{10,9},{11,10},{12... | collective-permute-start | bytes 3080 | tf_op jit(solution)/shard_map/ppermute | solution.py:20
  24.1 5.3 %collective-permute-start.7 = (f32[256,1]{1,0:T(8,128)S(1)}, f32[256,1]{1,0:T(8,128)S(1)}, u32[]{:S(2)}, u32[]{:S(2)}) collective-permute-start(f32[256,1]{1,0:T(8,128)S(1)} %get-tuple-element.134), channel_id=1, source_target_pairs={{0,1},{1,2},{2,3},{3,4},{4,5},{5,6},{6,7},{8,9},{9,10},{10,11},{11... | collective-permute-start | bytes 3080 | tf_op jit(solution)/shard_map/ppermute | solution.py:19
  31.5 13.5 %collective-permute-start.10 = (f32[256,1]{1,0:T(8,128)S(1)}, f32[256,1]{1,0:T(8,128)S(1)}, u32[]{:S(2)}, u32[]{:S(2)}) collective-permute-start(f32[256,1]{1,0:T(8,128)S(1)} %get-tuple-element.131), channel_id=1, source_target_pairs={{1,0},{2,1},{3,2},{4,3},{5,4},{6,5},{7,6},{9,8},{10,9},{11,10},{12... | collective-permute-start | bytes 3080 | tf_op jit(solution)/shard_map/ppermute | solution.py:20
  32.8 12.2 %collective-permute-start.11 = (f32[256,1]{1,0:T(8,128)S(1)}, f32[256,1]{1,0:T(8,128)S(1)}, u32[]{:S(2)}, u32[]{:S(2)}) collective-permute-start(f32[256,1]{1,0:T(8,128)S(1)} %get-tuple-element.130), channel_id=1, source_target_pairs={{0,1},{1,2},{2,3},{3,4},{4,5},{5,6},{6,7},{8,9},{9,10},{10,11},{11... | collective-permute-start | bytes 3080 | tf_op jit(solution)/shard_map/ppermute | solution.py:19
  39.2 5.9 %collective-permute-start.8 = (f32[1,512]{1,0:T(1,128)S(1)}, f32[1,512]{1,0:T(1,128)S(1)}, u32[]{:S(2)}, u32[]{:S(2)}) collective-permute-start(f32[1,512]{1,0:T(1,128)S(1)} %get-tuple-element.132), channel_id=1, source_target_pairs={{8,0},{16,8},{24,16},{32,24},{40,32},{48,40},{56,48},{64,56},{72,6... | collective-permute-start | bytes 6152 | tf_op jit(solution)/shard_map/ppermute | solution.py:20
  40.5 5.8 %collective-permute-start.9 = (f32[1,512]{1,0:T(1,128)S(1)}, f32[1,512]{1,0:T(1,128)S(1)}, u32[]{:S(2)}, u32[]{:S(2)}) collective-permute-start(f32[1,512]{1,0:T(1,128)S(1)} %get-tuple-element.133), channel_id=1, source_target_pairs={{0,8},{8,16},{16,24},{24,32},{32,40},{40,48},{48,56},{56,64},{64,7... | collective-permute-start | bytes 6152 | tf_op jit(solution)/shard_map/ppermute | solution.py:19
  47.2 16.7 %collective-permute-start.14 = (f32[256,1]{1,0:T(8,128)S(1)}, f32[256,1]{1,0:T(8,128)S(1)}, u32[]{:S(2)}, u32[]{:S(2)}) collective-permute-start(f32[256,1]{1,0:T(8,128)S(1)} %get-tuple-element.127), channel_id=1, source_target_pairs={{1,0},{2,1},{3,2},{4,3},{5,4},{6,5},{7,6},{9,8},{10,9},{11,10},{12... | collective-permute-start | bytes 3080 | tf_op jit(solution)/shard_map/ppermute | solution.py:20
  48.5 15.5 %collective-permute-start.15 = (f32[256,1]{1,0:T(8,128)S(1)}, f32[256,1]{1,0:T(8,128)S(1)}, u32[]{:S(2)}, u32[]{:S(2)}) collective-permute-start(f32[256,1]{1,0:T(8,128)S(1)} %get-tuple-element.126), channel_id=1, source_target_pairs={{0,1},{1,2},{2,3},{3,4},{4,5},{5,6},{6,7},{8,9},{9,10},{10,11},{11... | collective-permute-start | bytes 3080 | tf_op jit(solution)/shard_map/ppermute | solution.py:19
  52.6 11.4 %collective-permute-start.12 = (f32[1,512]{1,0:T(1,128)S(1)}, f32[1,512]{1,0:T(1,128)S(1)}, u32[]{:S(2)}, u32[]{:S(2)}) collective-permute-start(f32[1,512]{1,0:T(1,128)S(1)} %get-tuple-element.128), channel_id=1, source_target_pairs={{8,0},{16,8},{24,16},{32,24},{40,32},{48,40},{56,48},{64,56},{72,6... | collective-permute-start | bytes 6152 | tf_op jit(solution)/shard_map/ppermute | solution.py:20
  53.9 10.1 %collective-permute-start.13 = (f32[1,512]{1,0:T(1,128)S(1)}, f32[1,512]{1,0:T(1,128)S(1)}, u32[]{:S(2)}, u32[]{:S(2)}) collective-permute-start(f32[1,512]{1,0:T(1,128)S(1)} %get-tuple-element.129), channel_id=1, source_target_pairs={{0,8},{8,16},{16,24},{24,32},{32,40},{40,48},{48,56},{56,64},{64,7... | collective-permute-start | bytes 6152 | tf_op jit(solution)/shard_map/ppermute | solution.py:19
  64.8 0.8 copy-start.3
  64.8 35.8 %copy-start.2 = (s32[1024,512]{1,0:T(8,128)S(1)}, s32[1024,512]{1,0:T(8,128)}, u32[]{:S(2)}) copy-start(s32[1024,512]{1,0:T(8,128)} %param.13) | copy-start | bytes 6291460
  67.6 29.3 %all-to-all-start.2 = ((f32[128,4,128]{2,1,0:T(4,128)}), f32[128,4,128]{2,1,0:T(4,128)S(1)}, u32[]{:S(2)}, u32[]{:S(2)}) async-start(f32[128,4,128]{2,1,0:T(4,128)} %stack.17), calls=%async_computation.2 | async-start | bytes 524288 | tf_op jit(solution)/shard_map/all_to_all | solution.py:87
  97.0 25.5 %copy-start.4 = (f32[128,4,128]{2,1,0:T(4,128)}, f32[128,4,128]{2,1,0:T(4,128)S(1)}, u32[]{:S(2)}) copy-start(f32[128,4,128]{2,1,0:T(4,128)S(1)} %all-to-all-done.2) | copy-start | bytes 786436
  97.0 21.6 %all-to-all-start.1 = ((bf16[1024,16,32]{0,2,1:T(8,128)(2,1)}), bf16[1024,16,32]{0,2,1:T(8,128)(2,1)S(1)}, u32[]{:S(2)}, u32[]{:S(2)}) async-start(bf16[1024,16,32]{0,2,1:T(8,128)(2,1)} %bitcast.3), calls=%async_computation.1 | async-start | bytes 2097152 | tf_op jit(solution)/shard_map/all_to_all | solution.py:88
  118.6 32.0 %all-to-all-start = ((s32[1024,16,32]{0,2,1:T(8,128)}), s32[1024,16,32]{0,2,1:T(8,128)S(1)}, u32[]{:S(2)}, u32[]{:S(2)}) async-start(s32[1024,16,32]{0,2,1:T(8,128)} %bitcast), calls=%async_computation | async-start | bytes 4194304 | tf_op jit(solution)/shard_map/all_to_all | solution.py:89
  153.2 3.1 %copy-start.5 = (f32[16,2,2048]{2,1,0:T(2,128)S(1)}, f32[16,2,2048]{2,1,0:T(2,128)}, u32[]{:S(2)}) copy-start(f32[16,2,2048]{2,1,0:T(2,128)} %custom-call.8) | copy-start | bytes 786436
